TPU v7x, 32 devices: a whole 2x2x4 slice. The times are simulated.
32 devices in a mesh: dp: 16 (over z, y, core), expert: 2 (over x).
Axes of the slice: x: 2, y: 2, z: 4, core: 2. Of those that a mesh axis runs over, the one named last changes fastest.
Arguments:
- tokens: bfloat16 [256, 6144], P('dp', 'expert'), may hold values from -6 to 6
- expert_ids: int32 [256, 2], P('dp'), may hold values from 0 to 7, all different within a row; in each aligned block of 16 rows (0 to 15, 16 to 31, ...) at most 8 rows name the same one
- gate_probs: float32 [256, 2], P('dp'), may hold values from 0.1 to 1
- w_gate: bfloat16 [8, 6144, 8192], P('expert', None, 'dp'), may hold values from -0.078125 to 0.078125
- w_up: bfloat16 [8, 6144, 8192], P('expert', None, 'dp'), may hold values from -0.078125 to 0.078125
- w_down_t: bfloat16 [8, 6144, 8192], P('expert', 'dp'), may hold values from -0.0625 to 0.0625
Outputs:
- mixed: bfloat16 [256, 6144], P('dp', 'expert')
Inputs may be any that keep to these rules, and one draw needn't show every extreme that they name: `expert_ids`: each row names 2 different experts. Among the 16 rows of one index of dp no expert is named more than 8 times, a bound that some block reaches.
All inputs are finite; a program needn't handle non-finite values.
Results may differ from a plain program's by a relative error of at most 0.0057.
Values may be sent and summed in bfloat16 or wider, within the bound.
A program may use at most 128 MiB of HBM per device.

v0:
```python
import jax
import jax.numpy as jnp
from jax import lax
from jax.sharding import PartitionSpec as P


def assignments(expert_ids, experts, capacity):
    flat = expert_ids.reshape(-1)
    onehot = (flat[:, None] == jnp.arange(experts, dtype=jnp.int32)[None, :]).astype(jnp.int32)
    earlier = jnp.cumsum(onehot, axis=0) - onehot
    position = jnp.sum(earlier * onehot, axis=1).reshape(expert_ids.shape)
    expert_hit = (
        expert_ids[:, :, None] == jnp.arange(experts, dtype=jnp.int32)[None, None, :]
    ).astype(jnp.float32)
    slot_hit = (
        position[:, :, None] == jnp.arange(capacity, dtype=jnp.int32)[None, None, :]
    ).astype(jnp.float32)
    return (expert_hit, slot_hit)


def per_device(tokens, expert_ids, gate_probs, w_gate, w_up, w_down_t):
    local_experts = w_gate.shape[0]
    expert_count = lax.axis_size("expert")
    dp_count = lax.axis_size("dp")
    experts = local_experts * expert_count
    capacity = tokens.shape[0] // 2
    expert_hit, slot_hit = assignments(expert_ids, experts, capacity)
    dispatch_map = jnp.einsum("tke,tkc->ect", expert_hit, slot_hit).astype(jnp.bfloat16)
    combine_map = jnp.einsum(
        "tk,tke,tkc->tec", gate_probs, expert_hit, slot_hit, precision=lax.Precision.HIGHEST
    )
    slots = jnp.einsum(
        "ect,td->ecd", dispatch_map, tokens, preferred_element_type=jnp.float32
    ).astype(jnp.bfloat16)
    arrived = lax.all_to_all(slots, "expert", split_axis=0, concat_axis=2, tiled=True)
    piece = lax.all_gather(arrived, "dp", axis=1, tiled=True)
    gate = jnp.einsum("erd,edf->erf", piece, w_gate, preferred_element_type=jnp.float32)
    up = jnp.einsum("erd,edf->erf", piece, w_up, preferred_element_type=jnp.float32)
    hidden = (jax.nn.silu(gate) * up).astype(jnp.bfloat16)
    partial_out = jnp.einsum(
        "erf,edf->erd",
        lax.all_gather(hidden, "dp", axis=2, tiled=True),
        w_down_t,
        preferred_element_type=jnp.float32,
    )
    results = partial_out.astype(jnp.bfloat16).reshape(
        local_experts, dp_count, capacity, w_down_t.shape[1]
    )
    results = lax.all_to_all(results, "dp", split_axis=1, concat_axis=3, tiled=True)
    results = results.reshape(local_experts, capacity, results.shape[3])
    slice_width = tokens.shape[1]
    outgoing = results.reshape(local_experts, capacity, expert_count, slice_width)
    returned = lax.all_to_all(outgoing, "expert", split_axis=2, concat_axis=0, tiled=True)
    returned = returned.reshape(experts, capacity, slice_width)
    mixed = jnp.einsum(
        "tec,ecd->td", combine_map, returned.astype(jnp.float32), precision=lax.Precision.HIGHEST
    )
    return mixed.astype(jnp.bfloat16)


def solution(mesh):
    placed = (
        P("dp", "expert"),
        P("dp", None),
        P("dp", None),
        P("expert", None, "dp"),
        P("expert", None, "dp"),
        P("expert", "dp", None),
    )
    return jax.shard_map(
        per_device, mesh=mesh, in_specs=placed, out_specs=P("dp", "expert"), check_vma=False
    )
```

profile of v0, /device:TPU:0, one launch (start us, length us, event | category | flops | bytes accessed | tf_op | source)
XLA Modules:
  0.0 233.5 jit_solution(2106220213072693453)
XLA Ops:
  6.5 0.0 copy-start
  6.5 0.0 all-gather.3.cloned.1.call-start
  6.5 0.8 copy.17
  7.3 0.1 eq.46
  7.4 0.1 fusion.7
  7.5 0.1 reduce_window_sum.11
  7.5 0.2 select_reduce_fusion
  7.7 0.1 eq.50
  7.8 0.3 fusion.3
  8.1 0.1 copy.20
  8.2 0.0 copy-done
  8.2 0.2 convolution_convert_fusion
  8.5 10.6 %all_to_all.48 = bf16[8,8,3072]{2,1,0:T(8,128)(2,1)S(1)} all-to-all(bf16[8,8,3072]{2,1,0:T(8,128)(2,1)S(1)} %convolution_convert_fusion), channel_id=1, replica_groups=mesh['dp'=16,'expert'=2] {'expert'}, dimensions={0} | all-to-all | bytes 786432 | tf_op jit(solution)/shard_map/all_to_all | solution.py:35
  19.1 0.8 copy.21
  19.9 0.0 all-gather.3.cloned.1.call-update
  19.9 0.0 all-gather.5.cloned.1.call-start
  19.9 62.0 %all-gather.3.cloned.1.call-done = bf16[4,128,6144]{2,1,0:T(8,128)(2,1)} async-done(((bf16[4,8,6144]{2,1,0:T(8,128)(2,1)}), bf16[4,128,6144]{2,1,0:T(8,128)(2,1)}) %all-gather.3.cloned.1.call-update) | async-done | bytes 6291472 | tf_op jit(solution)/shard_map/all_gather | solution.py:36
  81.9 0.0 copy-start.2
  81.9 11.9 %fusion.16 = f32[4,128,512]{2,1,0:T(8,128)S(1)} fusion(bf16[4,128,6144]{2,1,0:T(8,128)(2,1)} %all-gather.3.cloned.1.call-done, bf16[4,6144,512]{2,1,0:T(8,128)(2,1)} %param.9), kind=kOutput, calls=%fused_computation.25 | convolution fusion | flops 3221225472 | bytes 32505856 | tf_op jit(solution)/shard_map/erd,edf->erf/dot_general | solution.py:37
  93.8 0.0 copy-done.2
  93.9 0.0 copy-start.1
  93.9 12.6 %fusion.1 = bf16[4,128,512]{2,1,0:T(8,128)(2,1)} fusion(bf16[4,128,6144]{2,1,0:T(8,128)(2,1)S(1)} %copy-done.2, bf16[4,6144,512]{2,1,0:T(8,128)(2,1)} %param.10, f32[4,128,512]{2,1,0:T(8,128)S(1)} %fusion.16), kind=kOutput, calls=%fused_computation.4 | convolution fusion | flops 3222798336 | bytes 33030144 | tf_op jit(solution)/shard_map/erd,edf->erf/dot_general | solution.py:38
  106.4 0.0 copy-start.3
  106.4 0.0 all-gather.5.cloned.1.call-update
  106.5 76.5 %all-gather.5.cloned.1.call-done = bf16[4,128,8192]{2,1,0:T(8,128)(2,1)} async-done(((bf16[4,128,512]{2,1,0:T(8,128)(2,1)}), bf16[4,128,8192]{2,1,0:T(8,128)(2,1)}) %all-gather.5.cloned.1.call-update) | async-done | bytes 8388624 | tf_op jit(solution)/shard_map/all_gather | solution.py:42
  183.0 14.5 %fusion.2 = bf16[4,16,8,384]{3,2,1,0:T(8,128)(2,1)S(1)} fusion(bf16[4,128,8192]{2,1,0:T(8,128)(2,1)} %all-gather.5.cloned.1.call-done, bf16[4,384,8192]{2,1,0:T(8,128)(2,1)} %param.11), kind=kOutput, calls=%fused_computation.6 | convolution fusion | flops 3221422080 | bytes 33947648 | tf_op jit(solution)/shard_map/erf,edf->erd/dot_general | solution.py:40
  197.5 0.8 copy.22
  198.3 3.6 %all-to-all-start.1 = ((bf16[4,16,8,384]{3,2,0,1:T(8,128)(2,1)}), bf16[4,16,8,384]{3,2,0,1:T(8,128)(2,1)S(1)}, u32[]{:S(2)}, u32[]{:S(2)}) async-start(bf16[4,16,8,384]{3,2,0,1:T(8,128)(2,1)} %copy.22), calls=%async_computation.1 | async-start | bytes 786432 | tf_op jit(solution)/shard_map/all_to_all | solution.py:49
  201.8 0.0 copy-done.3
  201.8 0.1 copy.18
  201.9 12.0 %all-to-all-done.1 = bf16[4,16,8,384]{3,2,0,1:T(8,128)(2,1)S(1)} async-done(((bf16[4,16,8,384]{3,2,0,1:T(8,128)(2,1)}), bf16[4,16,8,384]{3,2,0,1:T(8,128)(2,1)S(1)}, u32[]{:S(2)}, u32[]{:S(2)}) %all-to-all-start.1) | async-done | bytes 393248 | tf_op jit(solution)/shard_map/all_to_all | solution.py:49
  213.9 0.1 copy.23
  214.1 0.1 reshape_reshape.3
  214.2 0.8 copy.24
  215.0 3.5 %all-to-all-start.2 = ((bf16[4,8,2,3072]{3,1,0,2:T(8,128)(2,1)}), bf16[4,8,2,3072]{3,1,0,2:T(8,128)(2,1)S(1)}, u32[]{:S(2)}, u32[]{:S(2)}) async-start(bf16[4,8,2,3072]{3,1,0,2:T(8,128)(2,1)} %copy.24), calls=%async_computation.2 | async-start | bytes 786432 | tf_op jit(solution)/shard_map/all_to_all | solution.py:53
  218.5 0.4 fusion.6
  218.9 0.1 copy.26
  219.0 6.6 %all-to-all-done.2 = bf16[4,8,2,3072]{3,1,0,2:T(8,128)(2,1)S(1)} async-done(((bf16[4,8,2,3072]{3,1,0,2:T(8,128)(2,1)}), bf16[4,8,2,3072]{3,1,0,2:T(8,128)(2,1)S(1)}, u32[]{:S(2)}, u32[]{:S(2)}) %all-to-all-start.2) | async-done | bytes 393248 | tf_op jit(solution)/shard_map/all_to_all | solution.py:53
  225.6 1.1 fusion
  226.7 0.0 copy-done.1
Async XLA Ops:
  6.5 1.7 copy-start
  6.5 75.4 %all-gather.3.cloned.1.call-start = ((), (), s32[]{:S(2)}) async-start(), calls=%async_computation.3 | async-start | bytes 6684672 | tf_op jit(solution)/shard_map/all_gather | solution.py:36
  19.9 163.1 %all-gather.5.cloned.1.call-start = ((), (), s32[]{:S(2)}) async-start(), calls=%async_computation.4 | async-start | bytes 8912896 | tf_op jit(solution)/shard_map/all_gather | solution.py:42
  81.9 11.9 %copy-start.2 = (bf16[4,128,6144]{2,1,0:T(8,128)(2,1)S(1)}, bf16[4,128,6144]{2,1,0:T(8,128)(2,1)}, u32[]{:S(2)}) copy-start(bf16[4,128,6144]{2,1,0:T(8,128)(2,1)} %all-gather.3.cloned.1.call-done) | copy-start | bytes 18874372
  93.9 132.8 %copy-start.1 = (bf16[16,3072]{1,0:T(8,128)(2,1)S(1)}, bf16[16,3072]{1,0:T(8,128)(2,1)}, u32[]{:S(2)}) copy-start(bf16[16,3072]{1,0:T(8,128)(2,1)} %param.6) | copy-start | bytes 294916
  106.4 95.4 %copy-start.3 = (f32[16,2]{0,1:T(2,128)S(1)}, f32[16,2]{0,1:T(2,128)}, u32[]{:S(2)}) copy-start(f32[16,2]{0,1:T(2,128)} %param.8) | copy-start | bytes 388
  198.3 15.7 %all-to-all-start.1 = ((bf16[4,16,8,384]{3,2,0,1:T(8,128)(2,1)}), bf16[4,16,8,384]{3,2,0,1:T(8,128)(2,1)S(1)}, u32[]{:S(2)}, u32[]{:S(2)}) async-start(bf16[4,16,8,384]{3,2,0,1:T(8,128)(2,1)} %copy.22), calls=%async_computation.1 | async-start | bytes 786432 | tf_op jit(solution)/shard_map/all_to_all | solution.py:49
  215.0 10.6 %all-to-all-start.2 = ((bf16[4,8,2,3072]{3,1,0,2:T(8,128)(2,1)}), bf16[4,8,2,3072]{3,1,0,2:T(8,128)(2,1)S(1)}, u32[]{:S(2)}, u32[]{:S(2)}) async-start(bf16[4,8,2,3072]{3,1,0,2:T(8,128)(2,1)} %copy.24), calls=%async_computation.2 | async-start | bytes 786432 | tf_op jit(solution)/shard_map/all_to_all | solution.py:53
Sparse Core Ops, SparseCore 0:
  20.0 61.8 all-gather.2
  106.6 76.3 all-gather.4
where the time goes:
time: 234 us
  waiting for transfers between devices  157 us (67%)
  matrix products  41 us (18%)
  between operations  13.5 us (6%)
  blocking collectives  10.6 us (5%)
  starting transfers between devices  7.06 us (3%)
  local copies, waits for them, and re-layouts  3.83 us (2%)
    all_gather x1, waiting for transfers between devices, per_device(): lax.all_gather(hidden, 'dp', axis=2, tiled=True)  76.5 us
    all_gather x1, waiting for transfers between devices, per_device(): piece = lax.all_gather(arrived, 'dp', axis=1, tiled=True)  62 us
    dot_general x1, matrix products, per_device(): jnp.einsum('erf,edf->erd', lax.all_gather(hidden, 'dp', axis=2, tiled=Tru...  14.5 us
    dot_general x1, matrix products, per_device(): jnp.einsum('erd,edf->erf', piece, w_up, preferred_element_type=jnp.float32)  12.6 us
    all_to_all x1, waiting for transfers between devices, per_device(): lax.all_to_all(results, 'dp', split_axis=1, concat_axis=3, tiled=True)  12 us
    dot_general x1, matrix products, per_device(): jnp.einsum('erd,edf->erf', piece, w_gate, preferred_element_type=jnp.floa...  11.9 us
    all_to_all x1, blocking collectives, per_device(): lax.all_to_all(slots, 'expert', split_axis=0, concat_axis=2, tiled=True)  10.6 us
    all_to_all x1, waiting for transfers between devices, per_device(): lax.all_to_all(outgoing, 'expert', split_axis=2, concat_axis=0, tiled=True)  6.61 us
  transfers between devices with their start and end apart: 4, of which 4 were waited for; matrix products, arithmetic and copies ran while one was open for 0% of the time, Pallas kernels for 0%

commit v1 on v0

--- a/solution.py
+++ b/solution.py
@@ -37,12 +37,23 @@
     gate = jnp.einsum("erd,edf->erf", piece, w_gate, preferred_element_type=jnp.float32)
     up = jnp.einsum("erd,edf->erf", piece, w_up, preferred_element_type=jnp.float32)
     hidden = (jax.nn.silu(gate) * up).astype(jnp.bfloat16)
-    partial_out = jnp.einsum(
-        "erf,edf->erd",
-        lax.all_gather(hidden, "dp", axis=2, tiled=True),
-        w_down_t,
-        preferred_element_type=jnp.float32,
-    )
+    high = jax.lax.axis_size("dp")
+    block_out = jax.lax.axis_index("dp")
+    m_next, ready, block_now = (high, block_out, hidden.shape[2])
+    samples = tuple(((nth, (nth + 1) % m_next) for nth in range(m_next)))
+    current_value, partial_out = (hidden, None)
+    for h in tuple(range(m_next)):
+        current_arr = jax.lax.ppermute(current_value, "dp", samples) if h < m_next - 1 else None
+        last = jnp.einsum(
+            "erf,edf->erd",
+            current_value,
+            lax.dynamic_slice_in_dim(
+                w_down_t, (ready - h) % m_next * block_now, current_value.shape[2], axis=2
+            ),
+            preferred_element_type=jnp.float32,
+        )
+        partial_out = last if partial_out is None else partial_out + last
+        current_value = current_arr
     results = partial_out.astype(jnp.bfloat16).reshape(
         local_experts, dp_count, capacity, w_down_t.shape[1]
     )

time: 234 us -> 314 us (1.34)
  waiting for transfers between devices: 157 us -> 218 us
  matrix products: 41 us -> 58.7 us
    ppermute x0 -> x15, waiting for transfers between devices: none -> 137 us  [per_device(): jax.lax.ppermute(current_value, 'dp', samples)]
    all_gather x1 -> x0, waiting for transfers between devices: 76.5 us -> none  [per_device(): lax.all_gather(hidden, 'dp', axis=2, tiled=True)]
    dot_general x1 -> x16, matrix products: 14.5 us -> 33 us  [per_device(): jnp.einsum('erf,edf->erd', current_value, lax.dynamic_slice_in_dim(w_down...]
  transfers between devices with their start and end apart: 4 -> 18, of which waited for: 4 -> 18; matrix products, arithmetic and copies ran while one was open for 0% -> 10% of each run, Pallas kernels for 0% -> 0%
where the time goes in v1:
time: 314 us
  waiting for transfers between devices  218 us (69%)
  matrix products  58.7 us (19%)
  between operations  13.6 us (4%)
  blocking collectives  10.6 us (3%)
  starting transfers between devices  7.36 us (2%)
  local copies, waits for them, and re-layouts  5.46 us (2%)
    ppermute x15, waiting for transfers between devices, per_device(): jax.lax.ppermute(current_value, 'dp', samples)  137 us
    all_gather x1, waiting for transfers between devices, per_device(): piece = lax.all_gather(arrived, 'dp', axis=1, tiled=True)  62 us
    dot_general x16, matrix products, per_device(): jnp.einsum('erf,edf->erd', current_value, lax.dynamic_slice_in_dim(w_down...  33 us
    all_to_all x1, waiting for transfers between devices, per_device(): lax.all_to_all(results, 'dp', split_axis=1, concat_axis=3, tiled=True)  12 us
    dot_general x1, matrix products, per_device(): jnp.einsum('erd,edf->erf', piece, w_gate, preferred_element_type=jnp.floa...  11.9 us
    dot_general x1, matrix products, per_device(): jnp.einsum('erd,edf->erf', piece, w_up, preferred_element_type=jnp.float32)  11.7 us
    all_to_all x1, blocking collectives, per_device(): lax.all_to_all(slots, 'expert', split_axis=0, concat_axis=2, tiled=True)  10.6 us
    all_to_all x1, waiting for transfers between devices, per_device(): lax.all_to_all(outgoing, 'expert', split_axis=2, concat_axis=0, tiled=True)  6.61 us
  transfers between devices with their start and end apart: 18, of which 18 were waited for; matrix products, arithmetic and copies ran while one was open for 10% of the time, Pallas kernels for 0%

profile of v1, /device:TPU:0, one launch (start us, length us, event | category | flops | bytes accessed | tf_op | source)
XLA Modules:
  0.0 313.6 jit_solution(13014385433815353440)
XLA Ops:
  6.5 0.8 copy.17
  7.8 0.3 fusion.85
  8.5 10.6 %all_to_all.48 = bf16[8,8,3072]{2,1,0:T(8,128)(2,1)S(1)} all-to-all(bf16[8,8,3072]{2,1,0:T(8,128)(2,1)S(1)} %convolution_convert_fusion), channel_id=1, replica_groups=mesh['dp'=16,'expert'=2] {'expert'}, dimensions={0} | all-to-all | bytes 786432 | tf_op jit(solution)/shard_map/all_to_all | solution.py:35
  19.1 0.8 copy.21
  19.9 62.0 %all-gather.2.cloned.1.call-done = bf16[4,128,6144]{2,1,0:T(8,128)(2,1)} async-done(((bf16[4,8,6144]{2,1,0:T(8,128)(2,1)}), bf16[4,128,6144]{2,1,0:T(8,128)(2,1)}) %all-gather.2.cloned.1.call-update) | async-done | bytes 6291472 | tf_op jit(solution)/shard_map/all_gather | solution.py:36
  81.9 11.9 %fusion.114 = f32[4,128,512]{2,1,0:T(8,128)S(1)} fusion(bf16[4,128,6144]{2,1,0:T(8,128)(2,1)} %all-gather.2.cloned.1.call-done, bf16[4,6144,512]{2,1,0:T(8,128)(2,1)} %param.9), kind=kOutput, calls=%fused_computation.88 | convolution fusion | flops 3221225472 | bytes 32505856 | tf_op jit(solution)/shard_map/erd,edf->erf/dot_general | solution.py:37
  93.9 11.7 %fusion.78 = bf16[4,128,512]{2,1,0:T(8,128)(2,1)S(1)} fusion(bf16[4,128,6144]{2,1,0:T(8,128)(2,1)S(1)} %copy-done.2, bf16[4,6144,512]{2,1,0:T(8,128)(2,1)} %param.10, f32[4,128,512]{2,1,0:T(8,128)S(1)} %fusion.114), kind=kOutput, calls=%fused_computation.51 | convolution fusion | flops 3222798336 | bytes 33030144 | tf_op jit(solution)/shard_map/erd,edf->erf/dot_general | solution.py:38
  105.9 11.1 %collective-permute-done = bf16[4,128,512]{2,1,0:T(8,128)(2,1)S(1)} collective-permute-done((bf16[4,128,512]{2,1,0:T(8,128)(2,1)S(1)}, bf16[4,128,512]{2,1,0:T(8,128)(2,1)S(1)}, u32[]{:S(2)}, u32[]{:S(2)}) %collective-permute-start) | collective-permute-done | bytes 524320 | tf_op jit(solution)/shard_map/ppermute | solution.py:46
  116.9 11.3 %collective-permute-done.1 = bf16[4,128,512]{2,1,0:T(8,128)(2,1)S(1)} collective-permute-done((bf16[4,128,512]{2,1,0:T(8,128)(2,1)S(1)}, bf16[4,128,512]{2,1,0:T(8,128)(2,1)S(1)}, u32[]{:S(2)}, u32[]{:S(2)}) %collective-permute-start.1) | collective-permute-done | bytes 524320 | tf_op jit(solution)/shard_map/ppermute | solution.py:46
  128.2 0.8 copy-done.5
  129.0 10.5 %collective-permute-done.2 = bf16[4,128,512]{2,1,0:T(8,128)(2,1)S(1)} collective-permute-done((bf16[4,128,512]{2,1,0:T(8,128)(2,1)S(1)}, bf16[4,128,512]{2,1,0:T(8,128)(2,1)S(1)}, u32[]{:S(2)}, u32[]{:S(2)}) %collective-permute-start.2) | collective-permute-done | bytes 524320 | tf_op jit(solution)/shard_map/ppermute | solution.py:46
  139.5 11.3 %collective-permute-done.3 = bf16[4,128,512]{2,1,0:T(8,128)(2,1)S(1)} collective-permute-done((bf16[4,128,512]{2,1,0:T(8,128)(2,1)S(1)}, bf16[4,128,512]{2,1,0:T(8,128)(2,1)S(1)}, u32[]{:S(2)}, u32[]{:S(2)}) %collective-permute-start.3) | collective-permute-done | bytes 524320 | tf_op jit(solution)/shard_map/ppermute | solution.py:46
  150.8 0.8 copy-done.4
  151.6 10.5 %collective-permute-done.4 = bf16[4,128,512]{2,1,0:T(8,128)(2,1)S(1)} collective-permute-done((bf16[4,128,512]{2,1,0:T(8,128)(2,1)S(1)}, bf16[4,128,512]{2,1,0:T(8,128)(2,1)S(1)}, u32[]{:S(2)}, u32[]{:S(2)}) %collective-permute-start.4) | collective-permute-done | bytes 524320 | tf_op jit(solution)/shard_map/ppermute | solution.py:46
  162.1 11.3 %collective-permute-done.5 = bf16[4,128,512]{2,1,0:T(8,128)(2,1)S(1)} collective-permute-done((bf16[4,128,512]{2,1,0:T(8,128)(2,1)S(1)}, bf16[4,128,512]{2,1,0:T(8,128)(2,1)S(1)}, u32[]{:S(2)}, u32[]{:S(2)}) %collective-permute-start.5) | collective-permute-done | bytes 524320 | tf_op jit(solution)/shard_map/ppermute | solution.py:46
  173.5 11.3 %collective-permute-done.6 = bf16[4,128,512]{2,1,0:T(8,128)(2,1)S(1)} collective-permute-done((bf16[4,128,512]{2,1,0:T(8,128)(2,1)S(1)}, bf16[4,128,512]{2,1,0:T(8,128)(2,1)S(1)}, u32[]{:S(2)}, u32[]{:S(2)}) %collective-permute-start.6) | collective-permute-done | bytes 524320 | tf_op jit(solution)/shard_map/ppermute | solution.py:46
  184.8 2.0 fusion.31
  186.8 9.4 %collective-permute-done.7 = bf16[4,128,512]{2,1,0:T(8,128)(2,1)} collective-permute-done((bf16[4,128,512]{2,1,0:T(8,128)(2,1)S(1)}, bf16[4,128,512]{2,1,0:T(8,128)(2,1)}, u32[]{:S(2)}, u32[]{:S(2)}) %collective-permute-start.7) | collective-permute-done | bytes 524320 | tf_op jit(solution)/shard_map/ppermute | solution.py:46
  196.2 2.0 fusion.33
  198.2 2.2 fusion.36
  200.4 7.3 %collective-permute-done.8 = bf16[4,128,512]{2,1,0:T(8,128)(2,1)S(1)} collective-permute-done((bf16[4,128,512]{2,1,0:T(8,128)(2,1)}, bf16[4,128,512]{2,1,0:T(8,128)(2,1)S(1)}, u32[]{:S(2)}, u32[]{:S(2)}) %collective-permute-start.8) | collective-permute-done | bytes 524320 | tf_op jit(solution)/shard_map/ppermute | solution.py:46
  207.7 2.1 fusion.39
  209.7 2.2 fusion.42
  211.9 7.0 %collective-permute-done.9 = bf16[4,128,512]{2,1,0:T(8,128)(2,1)S(1)} collective-permute-done((bf16[4,128,512]{2,1,0:T(8,128)(2,1)S(1)}, bf16[4,128,512]{2,1,0:T(8,128)(2,1)S(1)}, u32[]{:S(2)}, u32[]{:S(2)}) %collective-permute-start.9) | collective-permute-done | bytes 524320 | tf_op jit(solution)/shard_map/ppermute | solution.py:46
  219.0 2.0 fusion.45
  221.0 2.2 fusion.48
  223.2 7.1 %collective-permute-done.10 = bf16[4,128,512]{2,1,0:T(8,128)(2,1)S(1)} collective-permute-done((bf16[4,128,512]{2,1,0:T(8,128)(2,1)S(1)}, bf16[4,128,512]{2,1,0:T(8,128)(2,1)S(1)}, u32[]{:S(2)}, u32[]{:S(2)}) %collective-permute-start.10) | collective-permute-done | bytes 524320 | tf_op jit(solution)/shard_map/ppermute | solution.py:46
  230.3 2.0 fusion.51
  232.3 2.2 fusion.54
  234.5 7.1 %collective-permute-done.11 = bf16[4,128,512]{2,1,0:T(8,128)(2,1)S(1)} collective-permute-done((bf16[4,128,512]{2,1,0:T(8,128)(2,1)S(1)}, bf16[4,128,512]{2,1,0:T(8,128)(2,1)S(1)}, u32[]{:S(2)}, u32[]{:S(2)}) %collective-permute-start.11) | collective-permute-done | bytes 524320 | tf_op jit(solution)/shard_map/ppermute | solution.py:46
  241.6 2.0 fusion.57
  243.6 2.0 fusion.60
  245.7 7.2 %collective-permute-done.12 = bf16[4,128,512]{2,1,0:T(8,128)(2,1)S(1)} collective-permute-done((bf16[4,128,512]{2,1,0:T(8,128)(2,1)S(1)}, bf16[4,128,512]{2,1,0:T(8,128)(2,1)S(1)}, u32[]{:S(2)}, u32[]{:S(2)}) %collective-permute-start.12) | collective-permute-done | bytes 524320 | tf_op jit(solution)/shard_map/ppermute | solution.py:46
  252.9 2.0 fusion.63
  254.9 2.0 fusion.66
  257.0 7.2 %collective-permute-done.13 = bf16[4,128,512]{2,1,0:T(8,128)(2,1)S(1)} collective-permute-done((bf16[4,128,512]{2,1,0:T(8,128)(2,1)S(1)}, bf16[4,128,512]{2,1,0:T(8,128)(2,1)S(1)}, u32[]{:S(2)}, u32[]{:S(2)}) %collective-permute-start.13) | collective-permute-done | bytes 524320 | tf_op jit(solution)/shard_map/ppermute | solution.py:46
  264.2 2.0 fusion.69
  266.2 2.0 fusion.72
  268.3 7.2 %collective-permute-done.14 = bf16[4,128,512]{2,1,0:T(8,128)(2,1)S(1)} collective-permute-done((bf16[4,128,512]{2,1,0:T(8,128)(2,1)S(1)}, bf16[4,128,512]{2,1,0:T(8,128)(2,1)S(1)}, u32[]{:S(2)}, u32[]{:S(2)}) %collective-permute-start.14) | collective-permute-done | bytes 524320 | tf_op jit(solution)/shard_map/ppermute | solution.py:46
  275.5 2.0 fusion.82
  277.5 0.8 copy.22
  278.3 3.6 %all-to-all-start.1 = ((bf16[4,16,8,384]{3,2,0,1:T(8,128)(2,1)}), bf16[4,16,8,384]{3,2,0,1:T(8,128)(2,1)S(1)}, u32[]{:S(2)}, u32[]{:S(2)}) async-start(bf16[4,16,8,384]{3,2,0,1:T(8,128)(2,1)} %copy.22), calls=%async_computation.1 | async-start | bytes 786432 | tf_op jit(solution)/shard_map/all_to_all | solution.py:60
  282.0 12.0 %all-to-all-done.1 = bf16[4,16,8,384]{3,2,0,1:T(8,128)(2,1)S(1)} async-done(((bf16[4,16,8,384]{3,2,0,1:T(8,128)(2,1)}), bf16[4,16,8,384]{3,2,0,1:T(8,128)(2,1)S(1)}, u32[]{:S(2)}, u32[]{:S(2)}) %all-to-all-start.1) | async-done | bytes 393248 | tf_op jit(solution)/shard_map/all_to_all | solution.py:60
  294.2 0.8 copy.24
  295.0 3.5 %all-to-all-start.2 = ((bf16[4,8,2,3072]{3,1,0,2:T(8,128)(2,1)}), bf16[4,8,2,3072]{3,1,0,2:T(8,128)(2,1)S(1)}, u32[]{:S(2)}, u32[]{:S(2)}) async-start(bf16[4,8,2,3072]{3,1,0,2:T(8,128)(2,1)} %copy.24), calls=%async_computation.2 | async-start | bytes 786432 | tf_op jit(solution)/shard_map/all_to_all | solution.py:64
  298.5 0.4 fusion.88
  299.0 6.6 %all-to-all-done.2 = bf16[4,8,2,3072]{3,1,0,2:T(8,128)(2,1)S(1)} async-done(((bf16[4,8,2,3072]{3,1,0,2:T(8,128)(2,1)}), bf16[4,8,2,3072]{3,1,0,2:T(8,128)(2,1)S(1)}, u32[]{:S(2)}, u32[]{:S(2)}) %all-to-all-start.2) | async-done | bytes 393248 | tf_op jit(solution)/shard_map/all_to_all | solution.py:64
  305.6 1.1 fusion
  (40 shorter events, 1.6 us)
Async XLA Ops:
  6.5 1.7 copy-start
  6.5 75.4 %all-gather.2.cloned.1.call-start = ((), (), s32[]{:S(2)}) async-start(), calls=%async_computation.3 | async-start | bytes 6684672 | tf_op jit(solution)/shard_map/all_gather | solution.py:36
  81.9 11.9 %copy-start.2 = (bf16[4,128,6144]{2,1,0:T(8,128)(2,1)S(1)}, bf16[4,128,6144]{2,1,0:T(8,128)(2,1)}, u32[]{:S(2)}) copy-start(bf16[4,128,6144]{2,1,0:T(8,128)(2,1)} %all-gather.2.cloned.1.call-done) | copy-start | bytes 18874372
  105.6 11.4 %collective-permute-start = (bf16[4,128,512]{2,1,0:T(8,128)(2,1)S(1)}, bf16[4,128,512]{2,1,0:T(8,128)(2,1)S(1)}, u32[]{:S(2)}, u32[]{:S(2)}) collective-permute-start(bf16[4,128,512]{2,1,0:T(8,128)(2,1)S(1)} %fusion.78), channel_id=1, source_target_pairs={{0,2},{2,4},{4,6},{6,8},{8,10},{10,12},{12,14},{14,16},{16,18},{18... | collective-permute-start | bytes 1572872 | tf_op jit(solution)/shard_map/ppermute | solution.py:46
  116.9 11.3 %collective-permute-start.1 = (bf16[4,128,512]{2,1,0:T(8,128)(2,1)S(1)}, bf16[4,128,512]{2,1,0:T(8,128)(2,1)S(1)}, u32[]{:S(2)}, u32[]{:S(2)}) collective-permute-start(bf16[4,128,512]{2,1,0:T(8,128)(2,1)S(1)} %collective-permute-done), channel_id=1, source_target_pairs={{0,2},{2,4},{4,6},{6,8},{8,10},{10,12},{12,14},{14,16},{16,18},{18... | collective-permute-start | bytes 1572872 | tf_op jit(solution)/shard_map/ppermute | solution.py:46
  128.2 0.8 copy-start.5
  128.2 11.3 %collective-permute-start.2 = (bf16[4,128,512]{2,1,0:T(8,128)(2,1)S(1)}, bf16[4,128,512]{2,1,0:T(8,128)(2,1)S(1)}, u32[]{:S(2)}, u32[]{:S(2)}) collective-permute-start(bf16[4,128,512]{2,1,0:T(8,128)(2,1)S(1)} %collective-permute-done.1), channel_id=1, source_target_pairs={{0,2},{2,4},{4,6},{6,8},{8,10},{10,12},{12,14},{14,16},{16,18},{18... | collective-permute-start | bytes 1572872 | tf_op jit(solution)/shard_map/ppermute | solution.py:46
  139.5 11.3 %collective-permute-start.3 = (bf16[4,128,512]{2,1,0:T(8,128)(2,1)S(1)}, bf16[4,128,512]{2,1,0:T(8,128)(2,1)S(1)}, u32[]{:S(2)}, u32[]{:S(2)}) collective-permute-start(bf16[4,128,512]{2,1,0:T(8,128)(2,1)S(1)} %collective-permute-done.2), channel_id=1, source_target_pairs={{0,2},{2,4},{4,6},{6,8},{8,10},{10,12},{12,14},{14,16},{16,18},{18... | collective-permute-start | bytes 1572872 | tf_op jit(solution)/shard_map/ppermute | solution.py:46
  150.8 0.8 copy-start.4
  150.8 11.3 %collective-permute-start.4 = (bf16[4,128,512]{2,1,0:T(8,128)(2,1)S(1)}, bf16[4,128,512]{2,1,0:T(8,128)(2,1)S(1)}, u32[]{:S(2)}, u32[]{:S(2)}) collective-permute-start(bf16[4,128,512]{2,1,0:T(8,128)(2,1)S(1)} %collective-permute-done.3), channel_id=1, source_target_pairs={{0,2},{2,4},{4,6},{6,8},{8,10},{10,12},{12,14},{14,16},{16,18},{18... | collective-permute-start | bytes 1572872 | tf_op jit(solution)/shard_map/ppermute | solution.py:46
  162.1 11.3 %collective-permute-start.5 = (bf16[4,128,512]{2,1,0:T(8,128)(2,1)S(1)}, bf16[4,128,512]{2,1,0:T(8,128)(2,1)S(1)}, u32[]{:S(2)}, u32[]{:S(2)}) collective-permute-start(bf16[4,128,512]{2,1,0:T(8,128)(2,1)S(1)} %collective-permute-done.4), channel_id=1, source_target_pairs={{0,2},{2,4},{4,6},{6,8},{8,10},{10,12},{12,14},{14,16},{16,18},{18... | collective-permute-start | bytes 1572872 | tf_op jit(solution)/shard_map/ppermute | solution.py:46
  173.4 11.3 %copy-start.3 = (bf16[4,128,512]{2,1,0:T(8,128)(2,1)}, bf16[4,128,512]{2,1,0:T(8,128)(2,1)S(1)}, u32[]{:S(2)}) copy-start(bf16[4,128,512]{2,1,0:T(8,128)(2,1)S(1)} %collective-permute-done.5) | copy-start | bytes 1572868
  173.4 11.3 %collective-permute-start.6 = (bf16[4,128,512]{2,1,0:T(8,128)(2,1)S(1)}, bf16[4,128,512]{2,1,0:T(8,128)(2,1)S(1)}, u32[]{:S(2)}, u32[]{:S(2)}) collective-permute-start(bf16[4,128,512]{2,1,0:T(8,128)(2,1)S(1)} %collective-permute-done.5), channel_id=1, source_target_pairs={{0,2},{2,4},{4,6},{6,8},{8,10},{10,12},{12,14},{14,16},{16,18},{18... | collective-permute-start | bytes 1572872 | tf_op jit(solution)/shard_map/ppermute | solution.py:46
  184.8 11.4 %collective-permute-start.7 = (bf16[4,128,512]{2,1,0:T(8,128)(2,1)S(1)}, bf16[4,128,512]{2,1,0:T(8,128)(2,1)}, u32[]{:S(2)}, u32[]{:S(2)}) collective-permute-start(bf16[4,128,512]{2,1,0:T(8,128)(2,1)S(1)} %collective-permute-done.6), channel_id=1, source_target_pairs={{0,2},{2,4},{4,6},{6,8},{8,10},{10,12},{12,14},{14,16},{16,18},{18... | collective-permute-start | bytes 1572872 | tf_op jit(solution)/shard_map/ppermute | solution.py:46
  196.2 11.5 %collective-permute-start.8 = (bf16[4,128,512]{2,1,0:T(8,128)(2,1)}, bf16[4,128,512]{2,1,0:T(8,128)(2,1)S(1)}, u32[]{:S(2)}, u32[]{:S(2)}) collective-permute-start(bf16[4,128,512]{2,1,0:T(8,128)(2,1)} %collective-permute-done.7), channel_id=1, source_target_pairs={{0,2},{2,4},{4,6},{6,8},{8,10},{10,12},{12,14},{14,16},{16,18},{18... | collective-permute-start | bytes 1572872 | tf_op jit(solution)/shard_map/ppermute | solution.py:46
  200.4 81.5 %copy-start.6 = (f32[16,2]{0,1:T(2,128)S(1)}, f32[16,2]{0,1:T(2,128)}, u32[]{:S(2)}) copy-start(f32[16,2]{0,1:T(2,128)} %param.8) | copy-start | bytes 388
  207.7 11.3 %collective-permute-start.9 = (bf16[4,128,512]{2,1,0:T(8,128)(2,1)S(1)}, bf16[4,128,512]{2,1,0:T(8,128)(2,1)S(1)}, u32[]{:S(2)}, u32[]{:S(2)}) collective-permute-start(bf16[4,128,512]{2,1,0:T(8,128)(2,1)S(1)} %collective-permute-done.8), channel_id=1, source_target_pairs={{0,2},{2,4},{4,6},{6,8},{8,10},{10,12},{12,14},{14,16},{16,18},{18... | collective-permute-start | bytes 1572872 | tf_op jit(solution)/shard_map/ppermute | solution.py:46
  207.7 99.1 %copy-start.1 = (bf16[16,3072]{1,0:T(8,128)(2,1)S(1)}, bf16[16,3072]{1,0:T(8,128)(2,1)}, u32[]{:S(2)}) copy-start(bf16[16,3072]{1,0:T(8,128)(2,1)} %param.6) | copy-start | bytes 294916
  219.0 11.3 %collective-permute-start.10 = (bf16[4,128,512]{2,1,0:T(8,128)(2,1)S(1)}, bf16[4,128,512]{2,1,0:T(8,128)(2,1)S(1)}, u32[]{:S(2)}, u32[]{:S(2)}) collective-permute-start(bf16[4,128,512]{2,1,0:T(8,128)(2,1)S(1)} %collective-permute-done.9), channel_id=1, source_target_pairs={{0,2},{2,4},{4,6},{6,8},{8,10},{10,12},{12,14},{14,16},{16,18},{18... | collective-permute-start | bytes 1572872 | tf_op jit(solution)/shard_map/ppermute | solution.py:46
  230.3 11.3 %collective-permute-start.11 = (bf16[4,128,512]{2,1,0:T(8,128)(2,1)S(1)}, bf16[4,128,512]{2,1,0:T(8,128)(2,1)S(1)}, u32[]{:S(2)}, u32[]{:S(2)}) collective-permute-start(bf16[4,128,512]{2,1,0:T(8,128)(2,1)S(1)} %collective-permute-done.10), channel_id=1, source_target_pairs={{0,2},{2,4},{4,6},{6,8},{8,10},{10,12},{12,14},{14,16},{16,18},{18... | collective-permute-start | bytes 1572872 | tf_op jit(solution)/shard_map/ppermute | solution.py:46
  241.6 11.3 %collective-permute-start.12 = (bf16[4,128,512]{2,1,0:T(8,128)(2,1)S(1)}, bf16[4,128,512]{2,1,0:T(8,128)(2,1)S(1)}, u32[]{:S(2)}, u32[]{:S(2)}) collective-permute-start(bf16[4,128,512]{2,1,0:T(8,128)(2,1)S(1)} %collective-permute-done.11), channel_id=1, source_target_pairs={{0,2},{2,4},{4,6},{6,8},{8,10},{10,12},{12,14},{14,16},{16,18},{18... | collective-permute-start | bytes 1572872 | tf_op jit(solution)/shard_map/ppermute | solution.py:46
  252.9 11.3 %collective-permute-start.13 = (bf16[4,128,512]{2,1,0:T(8,128)(2,1)S(1)}, bf16[4,128,512]{2,1,0:T(8,128)(2,1)S(1)}, u32[]{:S(2)}, u32[]{:S(2)}) collective-permute-start(bf16[4,128,512]{2,1,0:T(8,128)(2,1)S(1)} %collective-permute-done.12), channel_id=1, source_target_pairs={{0,2},{2,4},{4,6},{6,8},{8,10},{10,12},{12,14},{14,16},{16,18},{18... | collective-permute-start | bytes 1572872 | tf_op jit(solution)/shard_map/ppermute | solution.py:46
  264.2 11.3 %collective-permute-start.14 = (bf16[4,128,512]{2,1,0:T(8,128)(2,1)S(1)}, bf16[4,128,512]{2,1,0:T(8,128)(2,1)S(1)}, u32[]{:S(2)}, u32[]{:S(2)}) collective-permute-start(bf16[4,128,512]{2,1,0:T(8,128)(2,1)S(1)} %collective-permute-done.13), channel_id=1, source_target_pairs={{0,2},{2,4},{4,6},{6,8},{8,10},{10,12},{12,14},{14,16},{16,18},{18... | collective-permute-start | bytes 1572872 | tf_op jit(solution)/shard_map/ppermute | solution.py:46
  278.3 15.7 %all-to-all-start.1 = ((bf16[4,16,8,384]{3,2,0,1:T(8,128)(2,1)}), bf16[4,16,8,384]{3,2,0,1:T(8,128)(2,1)S(1)}, u32[]{:S(2)}, u32[]{:S(2)}) async-start(bf16[4,16,8,384]{3,2,0,1:T(8,128)(2,1)} %copy.22), calls=%async_computation.1 | async-start | bytes 786432 | tf_op jit(solution)/shard_map/all_to_all | solution.py:60
  295.0 10.6 %all-to-all-start.2 = ((bf16[4,8,2,3072]{3,1,0,2:T(8,128)(2,1)}), bf16[4,8,2,3072]{3,1,0,2:T(8,128)(2,1)S(1)}, u32[]{:S(2)}, u32[]{:S(2)}) async-start(bf16[4,8,2,3072]{3,1,0,2:T(8,128)(2,1)} %copy.24), calls=%async_computation.2 | async-start | bytes 786432 | tf_op jit(solution)/shard_map/all_to_all | solution.py:64
Sparse Core Ops, SparseCore 0:
  20.0 61.8 all-gather.1
